TPU v7x, 32 devices: a whole 2x2x4 slice. The times are simulated.
32 devices in a mesh: rp: 8 (over y, x, core), re: 4 (over z).
Axes of the slice: x: 2, y: 2, z: 4, core: 2. Of those that a mesh axis runs over, the one named last changes fastest.
Arguments:
- coupling: bfloat16 [128, 4, 2, 6, 4096], P('rp', 're'), may hold values from -1.25 to 1.25
- rp_coords: int32 [3, 128], P(None, 'rp'), may hold values from -8 to 8
- degeneracy: int32 [128], P('rp'), may hold values from 1 to 8
- qpoints: int32 [3, 64], replicated, may hold values from 0 to 15
- eigvec: float32 [64, 2, 6, 6], P('rp'), may hold values from -1.75 to 1.75
Outputs:
- coupling_q: float32 [64, 4, 2, 6, 4096], P('rp', None, None, None, 're')
All inputs are finite; a program needn't handle non-finite values.
Results may differ from a plain program's by a relative error of at most 0.0042.
Values may be sent and summed in bfloat16 or wider, within the bound.
A program may use at most 64 MiB of HBM per device.

v0:
```python
import math

import jax
import jax.numpy as jnp
from jax import lax
from jax.sharding import PartitionSpec as P

QGRID = 16


def phases(points, coords, degeneracy):
    turns = jnp.mod(points[0][:, None] * coords[0][None, :], QGRID)
    turns = turns + jnp.mod(points[1][:, None] * coords[1][None, :], QGRID)
    turns = turns + jnp.mod(points[2][:, None] * coords[2][None, :], QGRID)
    turns = jnp.mod(turns, QGRID)
    angles = turns.astype(jnp.float32) * (2.0 * math.pi / QGRID)
    weights = 1.0 / degeneracy.astype(jnp.float32)
    table = jnp.concatenate(
        [jnp.cos(angles) * weights[None, :], jnp.sin(angles) * weights[None, :]], axis=0
    )
    return table.astype(jnp.bfloat16)


def combine(table, coupling):
    point_count = table.shape[0] // 2
    product = jnp.dot(
        table, coupling.reshape(coupling.shape[0], -1), preferred_element_type=jnp.float32
    )
    product = product.reshape((2, point_count) + coupling.shape[1:])
    real_part = product[0, :, :, 0] - product[1, :, :, 1]
    imag_part = product[0, :, :, 1] + product[1, :, :, 0]
    return jnp.stack([real_part, imag_part], axis=2)


def mode_mix(values, matrix):
    return jnp.einsum("qrkp,qkn->qrnp", values, matrix, precision=lax.Precision.HIGHEST)


def rotate(summed, eigvec):
    real_in = summed[:, :, 0]
    imag_in = summed[:, :, 1]
    vec_real = eigvec[:, 0]
    vec_imag = eigvec[:, 1]
    real_out = mode_mix(real_in, vec_real) - mode_mix(imag_in, vec_imag)
    imag_out = mode_mix(real_in, vec_imag) + mode_mix(imag_in, vec_real)
    return jnp.stack([real_out, imag_out], axis=2)


def to_owners(all_points):
    return lax.all_to_all(all_points, "rp", split_axis=0, concat_axis=3, tiled=True)


def per_device(coupling, rp_coords, degeneracy, qpoints, eigvec):
    stacked = jnp.concatenate([rp_coords, degeneracy[None, :]], axis=0)
    lattice = lax.all_gather(stacked, "rp", axis=1, tiled=True)
    table = phases(qpoints, lattice[:3], lattice[3])
    rp_count = lax.axis_size("rp")
    re_count = lax.axis_size("re")
    local_rp, local_re, parts, mode_count, pair_count = coupling.shape
    q_local = eigvec.shape[0]
    pair_share = pair_count // re_count
    block_cols = mode_count * pair_share
    inner = block_cols // rp_count
    reordered = coupling.reshape(local_rp, local_re, parts, mode_count, re_count, pair_share)
    reordered = jnp.swapaxes(reordered, 3, 4)
    reordered = reordered.reshape(local_rp, local_re, parts, re_count, rp_count, inner)
    reordered = jnp.swapaxes(reordered, 3, 4)
    reordered = reordered.reshape(local_rp, local_re, parts, rp_count * re_count * inner)
    moved = lax.all_to_all(
        lax.all_to_all(reordered, "rp", split_axis=3, concat_axis=0, tiled=True),
        "re",
        split_axis=3,
        concat_axis=1,
        tiled=True,
    )
    all_points = combine(table, moved)
    summed = to_owners(all_points)
    summed = summed.reshape(q_local, summed.shape[1], parts, mode_count, pair_share)
    return rotate(summed, eigvec)


def solution(mesh):
    return jax.shard_map(
        per_device,
        mesh=mesh,
        in_specs=(
            P("rp", "re", None, None, None),
            P(None, "rp"),
            P("rp"),
            P(),
            P("rp", None, None, None),
        ),
        out_specs=P("rp", None, None, None, "re"),
        check_vma=False,
    )
```

profile of v0, /device:TPU:0, one launch (start us, length us, event | category | flops | bytes accessed | tf_op | source)
XLA Modules:
  0.0 183.5 jit_solution(7129110905378437116)
XLA Ops:
  0.0 3.7 %reshape.67 = bf16[16,1,2,6,4,1024]{5,4,2,3,0,1:T(4,128)(2,1)} reshape(bf16[16,1,2,6,4096]{4,2,3,1,0:T(2,128)(2,1)} %param.5) | data formatting | bytes 3145728 | tf_op jit(solution)/shard_map/reshape | solution.py:64
  3.7 2.5 %copy.92 = bf16[16,1,2,6,4,1024]{5,3,4,2,0,1:T(8,128)(2,1)S(1)} copy(bf16[16,1,2,6,4,1024]{5,4,2,3,0,1:T(4,128)(2,1)} %reshape.67) | data formatting | bytes 3145728 | tf_op jit(solution)/shard_map/reshape | solution.py:64
  6.2 1.9 %reshape.68 = bf16[16,1,2,4,8,768]{5,4,3,2,0,1:T(8,128)(2,1)} reshape(bf16[16,1,2,4,6,1024]{5,4,3,2,0,1:T(8,128)(2,1)S(1)} %bitcast.114) | data formatting | bytes 3145728 | tf_op jit(solution)/shard_map/reshape | solution.py:66
  8.1 18.7 %copy.76 = bf16[16,1,2,8,4,768]{0,2,5,4,3,1:T(2,128)(2,1)} copy(bf16[16,1,2,8,4,768]{5,3,4,2,0,1:T(8,128)(2,1)} %bitcast.115) | data formatting | bytes 3145728 | tf_op jit(solution)/shard_map/reshape | solution.py:68
  26.8 14.2 %reshape.78 = bf16[8,2,49152]{2,1,0:T(2,128)(2,1)S(1)} reshape(bf16[24576,1,2,16]{3,2,1,0:T(2,128)(2,1)} %bitcast.112) | data formatting | bytes 3145728
  41.0 25.9 %all_to_all.48 = bf16[8,2,49152]{2,1,0:T(2,128)(2,1)S(1)} all-to-all(bf16[8,2,49152]{2,1,0:T(2,128)(2,1)S(1)} %reshape.78), channel_id=1, replica_groups=mesh['rp'=8,'re'=4] {'rp'}, dimensions={0} | all-to-all | bytes 3145728 | tf_op jit(solution)/shard_map/all_to_all | solution.py:70
  67.0 10.3 %reshape.79 = bf16[24576,1,2,16]{3,2,1,0:T(2,128)(2,1)} reshape(bf16[8,2,49152]{2,1,0:T(2,128)(2,1)S(1)} %all_to_all.48) | data formatting | bytes 3145728
  77.3 23.6 %copy.78 = bf16[16,1,2,8,3072]{4,0,3,2,1:T(8,128)(2,1)S(1)} copy(bf16[16,1,2,8,3072]{0,2,4,3,1:T(2,128)(2,1)} %bitcast.113) | data formatting | bytes 3145728 | tf_op jit(solution)/shard_map/all_to_all | solution.py:70
  100.9 2.9 %copy.61 = bf16[128,1,2,3072]{0,2,1,3:T(2,128)(2,1)} copy(bf16[128,1,2,3072]{3,0,2,1:T(8,128)(2,1)S(1)} %bitcast.117) | data formatting | bytes 3145728 | tf_op jit(solution)/shard_map/all_to_all | solution.py:70
  103.8 5.0 %all-to-all-start.1 = ((bf16[128,1,2,3072]{0,2,1,3:T(2,128)(2,1)}), bf16[128,1,2,3072]{0,2,1,3:T(2,128)(2,1)S(1)}, u32[]{:S(2)}, u32[]{:S(2)}) async-start(bf16[128,1,2,3072]{0,2,1,3:T(2,128)(2,1)} %copy.61), calls=%async_computation.1 | async-start | bytes 3145728 | tf_op jit(solution)/shard_map/all_to_all | solution.py:69
  108.8 8.0 %all-gather = s32[8,16,4]{1,2,0:T(4,128)S(1)} all-gather(s32[1,16,4]{1,2,0:T(4,128)S(1)} %add_bitcast_fusion), channel_id=1, replica_groups=mesh['rp'=8,'re'=4] {'rp'}, dimensions={0}, use_global_device_ids=true | all-gather | bytes 2304 | tf_op jit(solution)/shard_map/all_gather | solution.py:55
  116.8 0.1 reshape.73
  116.9 0.3 multiply_convert_fusion.1
  117.2 28.0 %all-to-all-done.1 = bf16[128,1,2,3072]{0,2,1,3:T(2,128)(2,1)S(1)} async-done(((bf16[128,1,2,3072]{0,2,1,3:T(2,128)(2,1)}), bf16[128,1,2,3072]{0,2,1,3:T(2,128)(2,1)S(1)}, u32[]{:S(2)}, u32[]{:S(2)}) %all-to-all-start.1) | async-done | bytes 1572896 | tf_op jit(solution)/shard_map/all_to_all | solution.py:69
  145.2 0.2 copy.62
  145.4 0.6 fusion
  146.0 0.1 fusion.7
  146.1 0.1 fusion.9
  146.2 0.1 pad_maximum_fusion.1
  146.3 2.2 %copy.66 = f32[64,4,2,768]{3,1,2,0:T(4,128)} copy(f32[64,4,2,768]{3,0,1,2:T(8,128)S(1)} %pad_maximum_fusion.1) | data formatting | bytes 3145728 | tf_op jit(solution)/shard_map/stack | solution.py:32
  148.5 3.9 %all-to-all-start.2 = ((f32[64,4,2,768]{3,1,2,0:T(4,128)}), f32[64,4,2,768]{3,1,2,0:T(4,128)S(1)}, u32[]{:S(2)}, u32[]{:S(2)}) async-start(f32[64,4,2,768]{3,1,2,0:T(4,128)} %copy.66), calls=%async_computation.2 | async-start | bytes 3145728 | tf_op jit(solution)/shard_map/all_to_all | solution.py:50
  152.4 0.1 copy.83
  152.5 0.1 copy.85
  152.7 20.5 %all-to-all-done.2 = f32[64,4,2,768]{3,1,2,0:T(4,128)S(1)} async-done(((f32[64,4,2,768]{3,1,2,0:T(4,128)}), f32[64,4,2,768]{3,1,2,0:T(4,128)S(1)}, u32[]{:S(2)}, u32[]{:S(2)}) %all-to-all-start.2) | async-done | bytes 1572896 | tf_op jit(solution)/shard_map/all_to_all | solution.py:50
  173.1 2.1 %copy.93 = f32[8,8,4,2,768]{4,0,3,2,1:T(8,128)} copy(f32[8,8,4,2,768]{4,2,3,1,0:T(4,128)S(1)} %bitcast.116) | data formatting | bytes 3145728 | tf_op jit(solution)/shard_map/all_to_all | solution.py:50
  175.2 1.6 reshape.71
  176.7 1.0 fusion.6
  177.8 1.0 fusion.5
  178.8 1.0 fusion.4
  179.8 1.0 fusion.3
  180.9 0.2 pad_maximum_fusion
  181.1 2.4 %copy.72 = f32[8,4,2,6,1024]{4,2,3,1,0:T(2,128)} copy(f32[8,4,2,6,1024]{4,3,1,0,2:T(8,128)S(1)} %pad_maximum_fusion) | data formatting | bytes 3145728 | tf_op jit(solution)/shard_map/stack | solution.py:46
  (15 shorter events, 0.1 us)
Async XLA Ops:
  103.8 5.0 %copy-start.1 = (s32[3,16]{1,0:T(4,128)S(1)}, s32[3,16]{1,0:T(4,128)}, u32[]{:S(2)}) copy-start(s32[3,16]{1,0:T(4,128)} %param.6) | copy-start | bytes 580
  103.8 5.0 %copy-start.3 = (s32[16]{0:T(128)S(1)}, s32[16]{0:T(128)}, u32[]{:S(2)}) copy-start(s32[16]{0:T(128)} %param.7) | copy-start | bytes 196
  103.8 13.1 %copy-start.2 = (s32[3,64]{1,0:T(4,128)S(1)}, s32[3,64]{1,0:T(4,128)}, u32[]{:S(2)}) copy-start(s32[3,64]{1,0:T(4,128)} %param.8) | copy-start | bytes 2308
  103.8 41.4 %all-to-all-start.1 = ((bf16[128,1,2,3072]{0,2,1,3:T(2,128)(2,1)}), bf16[128,1,2,3072]{0,2,1,3:T(2,128)(2,1)S(1)}, u32[]{:S(2)}, u32[]{:S(2)}) async-start(bf16[128,1,2,3072]{0,2,1,3:T(2,128)(2,1)} %copy.61), calls=%async_computation.1 | async-start | bytes 3145728 | tf_op jit(solution)/shard_map/all_to_all | solution.py:69
  148.5 3.9 %copy-start = (f32[8,2,6,6]{0,1,3,2:T(2,128)S(1)}, f32[8,2,6,6]{0,1,3,2:T(2,128)}, u32[]{:S(2)}) copy-start(f32[8,2,6,6]{0,1,3,2:T(2,128)} %param.9) | copy-start | bytes 6916
  148.5 24.7 %all-to-all-start.2 = ((f32[64,4,2,768]{3,1,2,0:T(4,128)}), f32[64,4,2,768]{3,1,2,0:T(4,128)S(1)}, u32[]{:S(2)}, u32[]{:S(2)}) async-start(f32[64,4,2,768]{3,1,2,0:T(4,128)} %copy.66), calls=%async_computation.2 | async-start | bytes 3145728 | tf_op jit(solution)/shard_map/all_to_all | solution.py:50
where the time goes:
time: 186 us; the launch traced here: 184 us
  local copies, waits for them, and re-layouts  86.6 us (47%)
  waiting for transfers between devices  48.5 us (26%)
  blocking collectives  33.9 us (18%)
  starting transfers between devices  8.9 us (5%)
  matrix products  4.69 us (3%)
    all_to_all x1, waiting for transfers between devices, per_device(): lax.all_to_all(lax.all_to_all(reordered, 'rp', split_axis=3, concat_axis=...  28 us
    all_to_all x2, local copies, waits for them, and re-layouts, per_device(): lax.all_to_all(reordered, 'rp', split_axis=3, concat_axis=0, tiled=True)  26.5 us
    all_to_all x1, blocking collectives, per_device(): lax.all_to_all(reordered, 'rp', split_axis=3, concat_axis=0, tiled=True)  25.9 us
    unnamed x13, local copies, waits for them, and re-layouts  24.9 us
    all_to_all x1, waiting for transfers between devices, to_owners(): lax.all_to_all(all_points, 'rp', split_axis=0, concat_axis=3, tiled=True)  20.5 us
    reshape x1, local copies, waits for them, and re-layouts, per_device(): reordered.reshape(local_rp, local_re, parts, rp_count * re_count * inner)  18.7 us
    all_gather x1, blocking collectives, per_device(): lattice = lax.all_gather(stacked, 'rp', axis=1, tiled=True)  7.97 us
    reshape x2, local copies, waits for them, and re-layouts, per_device(): coupling.reshape(local_rp, local_re, parts, mode_count, re_count, pair_sh...  6.24 us
  transfers between devices with their start and end apart: 2, of which 2 were waited for; matrix products, arithmetic and copies ran while one was open for 0% of the time, Pallas kernels for 0%

commit v1 on v0

--- a/solution.py
+++ b/solution.py
@@ -1,11 +1,15 @@
+import functools
 import math
 
 import jax
 import jax.numpy as jnp
 from jax import lax
+from jax.experimental import pallas as pl
+from jax.experimental.pallas import tpu as pltpu
 from jax.sharding import PartitionSpec as P
 
 QGRID = 16
+MESH = pl.DeviceIdType.MESH
 
 
 def phases(points, coords, degeneracy):
@@ -79,9 +83,313 @@
     return rotate(summed, eigvec)
 
 
+def column_of(angle):
+    return [math.cos(2.0 * math.pi * (step - angle) / QGRID) for step in range(QGRID)]
+
+
+def pick(turns, values):
+    picked = jnp.full(turns.shape, values[0], jnp.float32)
+    for step in range(1, QGRID):
+        picked = jnp.where(turns == step, jnp.float32(values[step]), picked)
+    return picked
+
+
+def far_first(count):
+    return sorted(range(count), key=lambda offset: (-min(offset, count - offset), offset))
+
+
+def exchange_kernel(
+    n,
+    planes,
+    coupling,
+    block,
+    points,
+    out,
+    gathered,
+    blocks,
+    wide,
+    columns,
+    summed,
+    vectors,
+    turned,
+    outgoing,
+    own_sem,
+    block_send,
+    block_recv,
+    first_send,
+    first_recv,
+    second_send,
+    second_recv,
+):
+    me = lax.axis_index("rp")
+    plane = lax.axis_index("re")
+    local_rp, _, parts, modes, pairs = coupling.shape
+    share = pairs // planes
+    lanes = share // n
+    q_local = out.shape[0]
+    q_count = n * q_local
+    total_rp = n * local_rp
+    offsets = far_first(planes)
+
+    barrier = pltpu.get_barrier_semaphore()
+
+    def greet(index, carry):
+        pl.semaphore_signal(
+            barrier,
+            inc=1,
+            device_id={
+                "rp": lax.rem(me + lax.rem(index, n), n),
+                "re": lax.rem(plane + index // n, planes),
+            },
+            device_id_type=MESH,
+        )
+        return carry
+
+    lax.fori_loop(1, n * planes, greet, 0)
+    pl.semaphore_wait(barrier, n * planes - 1)
+
+    def peer(shift):
+        return lax.rem(me + shift, n)
+
+    def source(shift):
+        return lax.rem(me + n - shift, n)
+
+    def block_copy(shift, slot):
+        return pltpu.make_async_remote_copy(
+            src_ref=block,
+            dst_ref=blocks.at[slot],
+            send_sem=block_send.at[shift],
+            recv_sem=block_recv.at[slot],
+            device_id={"rp": peer(shift)},
+            device_id_type=MESH,
+        )
+
+    def piece(offset, owner):
+        target = lax.rem(plane + offset, planes)
+        start = pl.multiple_of(target * share + owner * lanes, lanes)
+        return coupling.at[:, 0, :, :, pl.ds(start, lanes)]
+
+    def first_copy(offset, shift, slot):
+        return pltpu.make_async_remote_copy(
+            src_ref=piece(offset, peer(shift)),
+            dst_ref=gathered.at[offset, slot],
+            send_sem=first_send.at[offset, shift],
+            recv_sem=first_recv.at[offset, slot],
+            device_id={"rp": peer(shift)},
+            device_id_type=MESH,
+        )
+
+    def own_copy(offset):
+        return pltpu.make_async_copy(
+            piece(offset, me), gathered.at[offset, me], own_sem.at[offset]
+        )
+
+    def arrival(offset, slot):
+        origin = lax.rem(plane + planes - offset, planes)
+        start = pl.multiple_of(slot * lanes, lanes)
+        return out.at[:, origin, :, :, pl.ds(start, lanes)]
+
+    def second_copy(offset, shift, slot):
+        start = pl.multiple_of(me * lanes, lanes)
+        return pltpu.make_async_remote_copy(
+            src_ref=outgoing.at[offset, pl.ds(peer(shift) * q_local, q_local)],
+            dst_ref=out.at[:, plane, :, :, pl.ds(start, lanes)],
+            send_sem=second_send.at[offset, shift],
+            recv_sem=second_recv.at[offset, slot],
+            device_id={"rp": peer(shift), "re": lax.rem(plane + offset, planes)},
+            device_id_type=MESH,
+        )
+
+    def second_wait(offset, shift):
+        return pltpu.make_async_remote_copy(
+            src_ref=outgoing.at[offset, pl.ds(0, q_local)],
+            dst_ref=arrival(offset, source(shift)),
+            send_sem=second_send.at[offset, shift],
+            recv_sem=second_recv.at[offset, source(shift)],
+            device_id={"rp": peer(shift), "re": lax.rem(plane + offset, planes)},
+            device_id_type=MESH,
+        )
+
+    def local_second():
+        return pltpu.make_async_copy(
+            outgoing.at[0, pl.ds(me * q_local, q_local)],
+            arrival(0, me),
+            own_sem.at[planes],
+        )
+
+    def send_first(offset):
+        for shift in range(1, n):
+            first_copy(offset, shift, me).start()
+        own_copy(offset).start()
+
+    own_block = pltpu.make_async_copy(block, blocks.at[me], own_sem.at[planes + 1])
+    own_block.start()
+    for shift in range(1, n):
+        block_copy(shift, me).start()
+    for offset in offsets[:2]:
+        send_first(offset)
+
+    own_block.wait()
+    for shift in range(1, n):
+        block_copy(shift, source(shift)).wait_recv()
+
+    rows = jnp.zeros((8, total_rp), jnp.float32)
+    for slot in range(n):
+        placed = blocks[slot, q_local:, :]
+        rows = rows + (pltpu.roll(placed, slot * local_rp, 1) if slot else placed)
+    grid = rows.astype(jnp.int32)
+    turns = jnp.zeros((q_count, total_rp), jnp.int32)
+    for axis in range(3):
+        turns = turns + ((points[:, axis : axis + 1] * grid[axis : axis + 1, :]) & (QGRID - 1))
+    turns = turns & (QGRID - 1)
+    weights = 1.0 / rows[3:4, :]
+    cos = (pick(turns, column_of(0.0)) * weights).astype(jnp.bfloat16)
+    sin = (pick(turns, column_of(QGRID / 4)) * weights).astype(jnp.bfloat16)
+    table = jnp.concatenate(
+        [jnp.concatenate([cos, -sin], axis=1), jnp.concatenate([sin, cos], axis=1)], axis=0
+    )
+
+    entries = parts * modes * modes
+
+    def spread(slot, carry):
+        held = blocks[slot, :q_local, :]
+        rows_at = pl.ds(pl.multiple_of(slot * q_local, q_local), q_local)
+        for entry in range(entries):
+            vectors[entry, rows_at, :] = jnp.broadcast_to(
+                held[:, entry : entry + 1], (q_local, lanes)
+            )
+        return carry
+
+    lax.fori_loop(0, n, spread, 0)
+
+    for turn, offset in enumerate(offsets):
+        own_copy(offset).wait()
+        for shift in range(1, n):
+            first_copy(offset, shift, source(shift)).wait_recv()
+
+        def widen(slot, carry, offset=offset):
+            wide[pl.ds(slot * local_rp, local_rp), :, :modes, :] = gathered[offset, slot].astype(
+                jnp.float32
+            )
+            return carry
+
+        lax.fori_loop(0, n, widen, 0)
+        for part in range(parts):
+            for mode in range(modes):
+                columns[
+                    part * total_rp : (part + 1) * total_rp, mode * lanes : (mode + 1) * lanes
+                ] = wide[:, part, mode, :].astype(jnp.bfloat16)
+        summed[...] = jnp.dot(table, columns[...], preferred_element_type=jnp.float32)
+
+        def rotate_rows(slot, carry):
+            start = pl.multiple_of(slot * q_local, q_local)
+            rows_at = pl.ds(start, q_local)
+            imag_at = pl.ds(q_count + start, q_local)
+            real_in = [summed[rows_at, k * lanes : (k + 1) * lanes] for k in range(modes)]
+            imag_in = [summed[imag_at, k * lanes : (k + 1) * lanes] for k in range(modes)]
+            for mode in range(modes):
+                real_out = jnp.zeros((q_local, lanes), jnp.float32)
+                imag_out = jnp.zeros((q_local, lanes), jnp.float32)
+                for k in range(modes):
+                    vec_real = vectors[k * modes + mode, rows_at, :]
+                    vec_imag = vectors[(modes + k) * modes + mode, rows_at, :]
+                    real_out += real_in[k] * vec_real - imag_in[k] * vec_imag
+                    imag_out += real_in[k] * vec_imag + imag_in[k] * vec_real
+                turned[rows_at, 0, mode, :] = real_out
+                turned[rows_at, 1, mode, :] = imag_out
+            return carry
+
+        lax.fori_loop(0, n, rotate_rows, 0)
+        outgoing[offset] = turned[:, :, :modes, :].astype(jnp.bfloat16)
+        for shift in range(n):
+            if offset == 0 and shift == 0:
+                local_second().start()
+            else:
+                second_copy(offset, shift, me).start()
+        if turn + 2 < planes:
+            send_first(offsets[turn + 2])
+
+    for shift in range(1, n):
+        block_copy(shift, me).wait_send()
+    for offset in offsets:
+        for shift in range(n):
+            if shift:
+                first_copy(offset, shift, me).wait_send()
+            if offset == 0 and shift == 0:
+                local_second().wait()
+            else:
+                second_copy(offset, shift, me).wait_send()
+                second_wait(offset, shift).wait_recv()
+
+
+def exchanged(coupling, rp_coords, degeneracy, qpoints, eigvec):
+    n = lax.axis_size("rp")
+    planes = lax.axis_size("re")
+    local_rp, local_re, parts, modes, pairs = coupling.shape
+    q_local = eigvec.shape[0]
+    lanes = pairs // planes // n
+    total_rp = local_rp * n
+    q_count = q_local * n
+    entries = parts * modes * modes
+    stacked = jnp.concatenate([rp_coords, degeneracy[None, :]], axis=0).astype(jnp.float32)
+    block = jnp.concatenate(
+        [
+            jnp.pad(eigvec.reshape(q_local, entries), ((0, 0), (0, total_rp - entries))),
+            jnp.pad(stacked, ((0, 8 - stacked.shape[0]), (0, total_rp - local_rp))),
+        ],
+        axis=0,
+    )
+    gathered = pl.pallas_call(
+        functools.partial(exchange_kernel, n, planes),
+        out_shape=jax.ShapeDtypeStruct((q_local, planes, parts, modes, pairs // planes), jnp.bfloat16),
+        in_specs=[
+            pl.BlockSpec(memory_space=pl.ANY),
+            pl.BlockSpec(memory_space=pl.ANY),
+            pl.BlockSpec(memory_space=pltpu.VMEM),
+        ],
+        out_specs=pl.BlockSpec(memory_space=pl.ANY),
+        scratch_shapes=[
+            pltpu.VMEM((planes, n, local_rp, parts, modes, lanes), jnp.bfloat16),
+            pltpu.VMEM((n, q_local + 8, total_rp), jnp.float32),
+            pltpu.VMEM((total_rp, parts, 8, lanes), jnp.float32),
+            pltpu.VMEM((parts * total_rp, modes * lanes), jnp.bfloat16),
+            pltpu.VMEM((2 * q_count, modes * lanes), jnp.float32),
+            pltpu.VMEM((entries, q_count, lanes), jnp.float32),
+            pltpu.VMEM((q_count, parts, 8, lanes), jnp.float32),
+            pltpu.VMEM((planes, q_count, parts, modes, lanes), jnp.bfloat16),
+            pltpu.SemaphoreType.DMA((planes + 2,)),
+            pltpu.SemaphoreType.DMA((n,)),
+            pltpu.SemaphoreType.DMA((n,)),
+            pltpu.SemaphoreType.DMA((planes, n)),
+            pltpu.SemaphoreType.DMA((planes, n)),
+            pltpu.SemaphoreType.DMA((planes, n)),
+            pltpu.SemaphoreType.DMA((planes, n)),
+        ],
+        compiler_params=pltpu.CompilerParams(collective_id=0, has_side_effects=True),
+    )(coupling, block, qpoints.T)
+    return gathered.astype(jnp.float32)
+
+
+def fits(n, planes, coupling, eigvec):
+    local_rp, local_re, parts, modes, pairs = coupling.shape
+    return (
+        local_re == 1
+        and parts * modes * modes <= local_rp * n == 128
+        and pairs // planes // n == 128
+        and eigvec.shape[0] == 8
+        and modes <= 8
+    )
+
+
+def either(coupling, rp_coords, degeneracy, qpoints, eigvec):
+    if fits(lax.axis_size("rp"), lax.axis_size("re"), coupling, eigvec):
+        return exchanged(coupling, rp_coords, degeneracy, qpoints, eigvec)
+    return per_device(coupling, rp_coords, degeneracy, qpoints, eigvec)
+
+
 def solution(mesh):
     return jax.shard_map(
-        per_device,
+        either,
         mesh=mesh,
         in_specs=(
             P("rp", "re", None, None, None),

time: 186 us -> 61.7 us (0.33); the launches traced: 184 us -> 61.3 us
  local copies, waits for them, and re-layouts: 86.6 us -> 9.33 us
  Pallas kernels: 0 us -> 50.7 us
  waiting for transfers between devices: 48.5 us -> 0 us
  blocking collectives: 33.9 us -> 0 us
  starting transfers between devices: 8.9 us -> 0 us
  matrix products: 4.69 us -> 0 us
    pallas_call x0 -> x1, Pallas kernels: none -> 50.7 us  [exchanged(): pl.pallas_call(functools.partial(exchange_kernel, n, planes), out_shape=j...]
    all_to_all x2 -> x0, waiting for transfers between devices: 48.5 us -> none  [the longest x1 28 us: per_device(): lax.all_to_all(lax.all_to_all(reordered, 'rp', split_axis=3, concat_axis=...]
    all_to_all x4 -> x0, local copies, waits for them, and re-layouts: 28.7 us -> none  [the longest x2 26.5 us: per_device(): lax.all_to_all(reordered, 'rp', split_axis=3, concat_axis=0, tiled=True)]
    reshape x5 -> x1, local copies, waits for them, and re-layouts: 28.4 us -> 0.09 us  [exchanged(): eigvec.reshape(q_local, entries)]
    all_to_all x1 -> x0, blocking collectives: 25.9 us -> none  [per_device(): lax.all_to_all(reordered, 'rp', split_axis=3, concat_axis=0, tiled=True)]
    unnamed x13 -> x3, local copies, waits for them, and re-layouts: 24.9 us -> 6.07 us
    all_to_all x2 -> x0, starting transfers between devices: 8.9 us -> none  [the longest x1 5 us: per_device(): lax.all_to_all(lax.all_to_all(reordered, 'rp', split_axis=3, concat_axis=...]
    all_gather x1 -> x0, blocking collectives: 7.97 us -> none  [per_device(): lattice = lax.all_gather(stacked, 'rp', axis=1, tiled=True)]
  transfers between devices with their start and end apart: 2 -> 0, of which waited for: 2 -> 0; matrix products, arithmetic and copies ran while one was open for 0% -> 0% of each run, Pallas kernels for 0% -> 0%
where the time goes in v1:
time: 61.7 us; the launch traced here: 61.3 us
  Pallas kernels  50.7 us (82%)
  local copies, waits for them, and re-layouts  9.33 us (15%)
  other arithmetic  1.31 us (2%)
    pallas_call x1, Pallas kernels, exchanged(): pl.pallas_call(functools.partial(exchange_kernel, n, planes), out_shape=j...  50.7 us
    unnamed x3, local copies, waits for them, and re-layouts  6.07 us
    convert_element_type x1, local copies, waits for them, and re-layouts, exchanged(): return gathered.astype(jnp.float32)  3.18 us

profile of v1, /device:TPU:0, one launch (start us, length us, event | category | flops | bytes accessed | tf_op | source)
XLA Modules:
  0.0 61.3 jit_solution(10098088101627615193)
XLA Ops:
  0.0 0.7 %add_convert_fusion = f32[4,16]{1,0:T(4,128)S(1)} fusion(s32[1,16]{1,0:T(1,128)} %bitcast.3, s32[3,16]{1,0:T(4,128)} %param.6), kind=kLoop, calls=%fused_computation.3 | loop fusion | flops 128 | bytes 512 | tf_op jit(solution)/shard_map/convert_element_type | solution.py:334
  0.7 1.4 %copy.15 = s32[3,64]{0,1:T(8,128)} copy(s32[3,64]{1,0:T(4,128)} %param.8) | data formatting | bytes 1536 | tf_op args[3]
  2.1 0.9 %copy.14 = f32[8,2,6,6]{3,2,1,0:T(8,128)S(1)} copy(f32[8,2,6,6]{0,1,3,2:T(2,128)} %param.9) | data formatting | bytes 4608 | tf_op args[4]
  3.0 0.1 reshape.3
  3.1 0.6 select_maximum_fusion.block
  3.7 3.8 %copy.16.coupling = bf16[16,1,2,6,4096]{4,3,2,1,0:T(8,128)(2,1)} copy(bf16[16,1,2,6,4096]{4,2,3,1,0:T(2,128)(2,1)} %param.5) | data formatting | bytes 3145728 | tf_op args[0]
  7.5 50.7 %shard_map.55 = bf16[8,4,2,6,1024]{4,3,2,1,0:T(8,128)(2,1)} custom-call(bf16[16,1,2,6,4096]{4,3,2,1,0:T(8,128)(2,1)} %copy.16.coupling, f32[16,128]{1,0:T(8,128)} %select_maximum_fusion.block, s32[64,3]{1,0:T(8,128)} %bitcast.2), custom_call_target="tpu_custom_call" | custom-call | tf_op jit(solution)/shard_map/pallas_call | solution.py:342
  58.2 3.2 %copy.17 = f32[8,4,2,6,1024]{4,2,3,1,0:T(2,128)} copy(bf16[8,4,2,6,1024]{4,3,2,1,0:T(8,128)(2,1)} %shard_map.55) | data formatting | bytes 2359296 | tf_op jit(solution)/shard_map/convert_element_type | solution.py:370

commit v2 on v1

--- a/solution.py
+++ b/solution.py
@@ -107,8 +107,6 @@
     out,
     gathered,
     blocks,
-    wide,
-    columns,
     summed,
     vectors,
     turned,
@@ -123,11 +121,12 @@
 ):
     me = lax.axis_index("rp")
     plane = lax.axis_index("re")
-    local_rp, _, parts, modes, pairs = coupling.shape
+    local_rp, modes, parts, pairs = coupling.shape
     share = pairs // planes
     lanes = share // n
-    q_local = out.shape[0]
+    q_local = block.shape[0] - 8
     q_count = n * q_local
+    q_rows = q_local * modes * parts
     total_rp = n * local_rp
     offsets = far_first(planes)
 
@@ -164,36 +163,42 @@
             device_id_type=MESH,
         )
 
-    def piece(offset, owner):
+    def piece(offset, owner, mode):
         target = lax.rem(plane + offset, planes)
         start = pl.multiple_of(target * share + owner * lanes, lanes)
-        return coupling.at[:, 0, :, :, pl.ds(start, lanes)]
-
-    def first_copy(offset, shift, slot):
+        return coupling.at[:, mode, :, pl.ds(start, lanes)]
+
+    def landing(offset, slot, mode):
+        return gathered.at[offset, mode, pl.ds(slot * local_rp, local_rp)]
+
+    def first_copy(offset, shift, slot, mode):
         return pltpu.make_async_remote_copy(
-            src_ref=piece(offset, peer(shift)),
-            dst_ref=gathered.at[offset, slot],
-            send_sem=first_send.at[offset, shift],
-            recv_sem=first_recv.at[offset, slot],
+            src_ref=piece(offset, peer(shift), mode),
+            dst_ref=landing(offset, slot, mode),
+            send_sem=first_send.at[offset, shift, mode],
+            recv_sem=first_recv.at[offset, slot, mode],
             device_id={"rp": peer(shift)},
             device_id_type=MESH,
         )
 
-    def own_copy(offset):
+    def own_copy(offset, mode):
         return pltpu.make_async_copy(
-            piece(offset, me), gathered.at[offset, me], own_sem.at[offset]
-        )
+            piece(offset, me, mode), landing(offset, me, mode), own_sem.at[offset * modes + mode]
+        )
+
+    def leaving(offset, owner):
+        return outgoing.at[offset, pl.ds(owner * q_local, q_local)]
+
+    def home(origin, slot):
+        return out.at[:, origin, :, :, pl.ds(pl.multiple_of(slot * lanes, lanes), lanes)]
 
     def arrival(offset, slot):
-        origin = lax.rem(plane + planes - offset, planes)
-        start = pl.multiple_of(slot * lanes, lanes)
-        return out.at[:, origin, :, :, pl.ds(start, lanes)]
+        return home(lax.rem(plane + planes - offset, planes), slot)
 
     def second_copy(offset, shift, slot):
-        start = pl.multiple_of(me * lanes, lanes)
         return pltpu.make_async_remote_copy(
-            src_ref=outgoing.at[offset, pl.ds(peer(shift) * q_local, q_local)],
-            dst_ref=out.at[:, plane, :, :, pl.ds(start, lanes)],
+            src_ref=leaving(offset, peer(shift)),
+            dst_ref=home(plane, me),
             send_sem=second_send.at[offset, shift],
             recv_sem=second_recv.at[offset, slot],
             device_id={"rp": peer(shift), "re": lax.rem(plane + offset, planes)},
@@ -202,7 +207,7 @@
 
     def second_wait(offset, shift):
         return pltpu.make_async_remote_copy(
-            src_ref=outgoing.at[offset, pl.ds(0, q_local)],
+            src_ref=leaving(offset, peer(shift)),
             dst_ref=arrival(offset, source(shift)),
             send_sem=second_send.at[offset, shift],
             recv_sem=second_recv.at[offset, source(shift)],
@@ -212,17 +217,16 @@
 
     def local_second():
         return pltpu.make_async_copy(
-            outgoing.at[0, pl.ds(me * q_local, q_local)],
-            arrival(0, me),
-            own_sem.at[planes],
+            leaving(0, me), arrival(0, me), own_sem.at[planes * modes]
         )
 
     def send_first(offset):
-        for shift in range(1, n):
-            first_copy(offset, shift, me).start()
-        own_copy(offset).start()
-
-    own_block = pltpu.make_async_copy(block, blocks.at[me], own_sem.at[planes + 1])
+        for mode in range(modes):
+            for shift in range(1, n):
+                first_copy(offset, shift, me, mode).start()
+            own_copy(offset, mode).start()
+
+    own_block = pltpu.make_async_copy(block, blocks.at[me], own_sem.at[planes * modes + 1])
     own_block.start()
     for shift in range(1, n):
         block_copy(shift, me).start()
@@ -237,17 +241,22 @@
     for slot in range(n):
         placed = blocks[slot, q_local:, :]
         rows = rows + (pltpu.roll(placed, slot * local_rp, 1) if slot else placed)
+    width = parts * total_rp
+    repeat = lax.broadcasted_iota(jnp.int32, (total_rp, width), 1) // parts
+    repeat = repeat == lax.broadcasted_iota(jnp.int32, (total_rp, width), 0)
+    rows = jnp.dot(rows, repeat.astype(jnp.float32), preferred_element_type=jnp.float32)
     grid = rows.astype(jnp.int32)
-    turns = jnp.zeros((q_count, total_rp), jnp.int32)
+    turns = jnp.zeros((q_count, width), jnp.int32)
     for axis in range(3):
         turns = turns + ((points[:, axis : axis + 1] * grid[axis : axis + 1, :]) & (QGRID - 1))
     turns = turns & (QGRID - 1)
     weights = 1.0 / rows[3:4, :]
-    cos = (pick(turns, column_of(0.0)) * weights).astype(jnp.bfloat16)
-    sin = (pick(turns, column_of(QGRID / 4)) * weights).astype(jnp.bfloat16)
+    cos = pick(turns, column_of(0.0)) * weights
+    sin = pick(turns, column_of(QGRID / 4)) * weights
+    real_part = lax.rem(lax.broadcasted_iota(jnp.int32, (q_count, width), 1), parts) == 0
     table = jnp.concatenate(
-        [jnp.concatenate([cos, -sin], axis=1), jnp.concatenate([sin, cos], axis=1)], axis=0
-    )
+        [jnp.where(real_part, cos, -sin), jnp.where(real_part, sin, cos)], axis=0
+    ).astype(jnp.bfloat16)
 
     entries = parts * modes * modes
 
@@ -263,23 +272,15 @@
     lax.fori_loop(0, n, spread, 0)
 
     for turn, offset in enumerate(offsets):
-        own_copy(offset).wait()
-        for shift in range(1, n):
-            first_copy(offset, shift, source(shift)).wait_recv()
-
-        def widen(slot, carry, offset=offset):
-            wide[pl.ds(slot * local_rp, local_rp), :, :modes, :] = gathered[offset, slot].astype(
-                jnp.float32
+        for mode in range(modes):
+            own_copy(offset, mode).wait()
+            for shift in range(1, n):
+                first_copy(offset, shift, source(shift), mode).wait_recv()
+            summed[:, mode * lanes : (mode + 1) * lanes] = jnp.dot(
+                table,
+                gathered[offset, mode].reshape(width, lanes),
+                preferred_element_type=jnp.float32,
             )
-            return carry
-
-        lax.fori_loop(0, n, widen, 0)
-        for part in range(parts):
-            for mode in range(modes):
-                columns[
-                    part * total_rp : (part + 1) * total_rp, mode * lanes : (mode + 1) * lanes
-                ] = wide[:, part, mode, :].astype(jnp.bfloat16)
-        summed[...] = jnp.dot(table, columns[...], preferred_element_type=jnp.float32)
 
         def rotate_rows(slot, carry):
             start = pl.multiple_of(slot * q_local, q_local)
@@ -295,12 +296,15 @@
                     vec_imag = vectors[(modes + k) * modes + mode, rows_at, :]
                     real_out += real_in[k] * vec_real - imag_in[k] * vec_imag
                     imag_out += real_in[k] * vec_imag + imag_in[k] * vec_real
-                turned[rows_at, 0, mode, :] = real_out
-                turned[rows_at, 1, mode, :] = imag_out
+                first_row = slot * q_rows + mode * parts
+                turned[pl.ds(first_row, q_local, stride=modes * parts), :] = real_out
+                turned[pl.ds(first_row + 1, q_local, stride=modes * parts), :] = imag_out
             return carry
 
         lax.fori_loop(0, n, rotate_rows, 0)
-        outgoing[offset] = turned[:, :, :modes, :].astype(jnp.bfloat16)
+        outgoing[offset] = (
+            turned[...].astype(jnp.bfloat16).reshape(q_count, modes, parts, lanes)
+        )
         for shift in range(n):
             if offset == 0 and shift == 0:
                 local_second().start()
@@ -314,7 +318,8 @@
     for offset in offsets:
         for shift in range(n):
             if shift:
-                first_copy(offset, shift, me).wait_send()
+                for mode in range(modes):
+                    first_copy(offset, shift, me, mode).wait_send()
             if offset == 0 and shift == 0:
                 local_second().wait()
             else:
@@ -341,7 +346,7 @@
     )
     gathered = pl.pallas_call(
         functools.partial(exchange_kernel, n, planes),
-        out_shape=jax.ShapeDtypeStruct((q_local, planes, parts, modes, pairs // planes), jnp.bfloat16),
+        out_shape=jax.ShapeDtypeStruct((q_local, planes, modes, parts, n * lanes), jnp.bfloat16),
         in_specs=[
             pl.BlockSpec(memory_space=pl.ANY),
             pl.BlockSpec(memory_space=pl.ANY),
@@ -349,25 +354,23 @@
         ],
         out_specs=pl.BlockSpec(memory_space=pl.ANY),
         scratch_shapes=[
-            pltpu.VMEM((planes, n, local_rp, parts, modes, lanes), jnp.bfloat16),
+            pltpu.VMEM((planes, modes, total_rp, parts, lanes), jnp.bfloat16),
             pltpu.VMEM((n, q_local + 8, total_rp), jnp.float32),
-            pltpu.VMEM((total_rp, parts, 8, lanes), jnp.float32),
-            pltpu.VMEM((parts * total_rp, modes * lanes), jnp.bfloat16),
-            pltpu.VMEM((2 * q_count, modes * lanes), jnp.float32),
+            pltpu.VMEM((parts * q_count, modes * lanes), jnp.float32),
             pltpu.VMEM((entries, q_count, lanes), jnp.float32),
-            pltpu.VMEM((q_count, parts, 8, lanes), jnp.float32),
-            pltpu.VMEM((planes, q_count, parts, modes, lanes), jnp.bfloat16),
-            pltpu.SemaphoreType.DMA((planes + 2,)),
+            pltpu.VMEM((q_count * modes * parts, lanes), jnp.float32),
+            pltpu.VMEM((planes, q_count, modes, parts, lanes), jnp.bfloat16),
+            pltpu.SemaphoreType.DMA((planes * modes + 2,)),
             pltpu.SemaphoreType.DMA((n,)),
             pltpu.SemaphoreType.DMA((n,)),
-            pltpu.SemaphoreType.DMA((planes, n)),
-            pltpu.SemaphoreType.DMA((planes, n)),
+            pltpu.SemaphoreType.DMA((planes, n, modes)),
+            pltpu.SemaphoreType.DMA((planes, n, modes)),
             pltpu.SemaphoreType.DMA((planes, n)),
             pltpu.SemaphoreType.DMA((planes, n)),
         ],
         compiler_params=pltpu.CompilerParams(collective_id=0, has_side_effects=True),
-    )(coupling, block, qpoints.T)
-    return gathered.astype(jnp.float32)
+    )(jnp.swapaxes(coupling[:, 0], 1, 2), block, qpoints.T)
+    return jnp.swapaxes(gathered, 2, 3).astype(jnp.float32)
 
 
 def fits(n, planes, coupling, eigvec):

time: 61.7 us -> 49.5 us (0.80)
  Pallas kernels: 50.7 us -> 42.3 us
  local copies, waits for them, and re-layouts: 9.33 us -> 2.38 us
  other arithmetic: 1.31 us -> 4.42 us
    pallas_call x1, Pallas kernels: 50.7 us -> 42.3 us  [exchanged(): pl.pallas_call(functools.partial(exchange_kernel, n, planes), out_shape=j...]
    unnamed x3 -> x2, local copies, waits for them, and re-layouts: 6.07 us -> 2.3 us
    convert_element_type x1 -> x0, local copies, waits for them, and re-layouts: 3.18 us -> none  [exchanged(): return gathered.astype(jnp.float32)]
    convert_element_type x0 -> x1, other arithmetic: none -> 3.12 us  [exchanged(): return jnp.swapaxes(gathered, 2, 3).astype(jnp.float32)]
where the time goes in v2:
time: 49.5 us; the launch traced here: 49.2 us
  Pallas kernels  42.3 us (85%)
  other arithmetic  4.42 us (9%)
  local copies, waits for them, and re-layouts  2.38 us (5%)
    pallas_call x1, Pallas kernels, exchanged(): pl.pallas_call(functools.partial(exchange_kernel, n, planes), out_shape=j...  42.3 us
    convert_element_type x1, other arithmetic, exchanged(): return jnp.swapaxes(gathered, 2, 3).astype(jnp.float32)  3.12 us
    unnamed x2, local copies, waits for them, and re-layouts  2.3 us

profile of v2, /device:TPU:0, one launch (start us, length us, event | category | flops | bytes accessed | tf_op | source)
XLA Modules:
  0.0 49.2 jit_solution(4814534210688800396)
XLA Ops:
  0.0 0.7 %add_convert_fusion = f32[4,16]{1,0:T(4,128)S(1)} fusion(s32[1,16]{1,0:T(1,128)} %bitcast.9, s32[3,16]{1,0:T(4,128)} %param.6), kind=kLoop, calls=%fused_computation.4 | loop fusion | flops 128 | bytes 512 | tf_op jit(solution)/shard_map/convert_element_type | solution.py:339
  0.7 1.4 %copy.9 = s32[3,64]{0,1:T(8,128)} copy(s32[3,64]{1,0:T(4,128)} %param.8) | data formatting | bytes 1536 | tf_op args[3]
  2.1 0.9 %copy.8 = f32[8,2,6,6]{3,2,1,0:T(8,128)S(1)} copy(f32[8,2,6,6]{0,1,3,2:T(2,128)} %param.9) | data formatting | bytes 4608 | tf_op args[4]
  3.0 0.1 reshape.3
  3.1 0.6 %select_maximum_fusion.block = f32[16,128]{1,0:T(8,128)} fusion(f32[4,16]{1,0:T(4,128)S(1)} %add_convert_fusion, f32[8,72]{1,0:T(8,128)S(1)} %reshape.3), kind=kLoop, calls=%fused_computation.1 | loop fusion | flops 10240 | bytes 10752 | tf_op jit(solution)/shard_map/concatenate | solution.py:340
  3.7 42.3 %shard_map.55 = bf16[8,4,6,2,1024]{4,3,2,1,0:T(2,128)(2,1)} custom-call(bf16[16,6,2,4096]{3,2,1,0:T(2,128)(2,1)} %bitcast.7, f32[16,128]{1,0:T(8,128)} %select_maximum_fusion.block, s32[64,3]{1,0:T(8,128)} %bitcast.8), custom_call_target="tpu_custom_call" | custom-call | tf_op jit(solution)/shard_map/pallas_call | solution.py:347
  46.0 3.1 %convert_bitcast_fusion = f32[8,4,2,6,1024]{4,2,3,1,0:T(2,128)} fusion(bf16[8,4,6,2,1024]{4,3,2,1,0:T(2,128)(2,1)} %shard_map.55), kind=kLoop, calls=%fused_computation | loop fusion | flops 393216 | bytes 2359296 | tf_op jit(solution)/shard_map/convert_element_type | solution.py:373

commit v3 on v2

--- a/solution.py
+++ b/solution.py
@@ -102,11 +102,15 @@
     n,
     planes,
     coupling,
-    block,
+    coords,
+    degeneracy,
+    eigvec,
     points,
     out,
     gathered,
-    blocks,
+    all_coords,
+    all_degeneracy,
+    all_eigvec,
     summed,
     vectors,
     turned,
@@ -124,7 +128,7 @@
     local_rp, modes, parts, pairs = coupling.shape
     share = pairs // planes
     lanes = share // n
-    q_local = block.shape[0] - 8
+    q_local = eigvec.shape[2]
     q_count = n * q_local
     q_rows = q_local * modes * parts
     total_rp = n * local_rp
@@ -153,15 +157,26 @@
     def source(shift):
         return lax.rem(me + n - shift, n)
 
-    def block_copy(shift, slot):
-        return pltpu.make_async_remote_copy(
-            src_ref=block,
-            dst_ref=blocks.at[slot],
-            send_sem=block_send.at[shift],
-            recv_sem=block_recv.at[slot],
-            device_id={"rp": peer(shift)},
-            device_id_type=MESH,
-        )
+    small = ((coords, all_coords), (degeneracy, all_degeneracy), (eigvec, all_eigvec))
+
+    def block_copies(shift, slot):
+        return [
+            pltpu.make_async_remote_copy(
+                src_ref=held,
+                dst_ref=full.at[slot],
+                send_sem=block_send.at[shift, index],
+                recv_sem=block_recv.at[slot, index],
+                device_id={"rp": peer(shift)},
+                device_id_type=MESH,
+            )
+            for index, (held, full) in enumerate(small)
+        ]
+
+    def own_blocks():
+        return [
+            pltpu.make_async_copy(held, full.at[me], own_sem.at[planes * modes + 1 + index])
+            for index, (held, full) in enumerate(small)
+        ]
 
     def piece(offset, owner, mode):
         target = lax.rem(plane + offset, planes)
@@ -226,31 +241,38 @@
                 first_copy(offset, shift, me, mode).start()
             own_copy(offset, mode).start()
 
-    own_block = pltpu.make_async_copy(block, blocks.at[me], own_sem.at[planes * modes + 1])
-    own_block.start()
     for shift in range(1, n):
-        block_copy(shift, me).start()
+        for copy in block_copies(shift, me):
+            copy.start()
+    for copy in own_blocks():
+        copy.start()
     for offset in offsets[:2]:
         send_first(offset)
 
-    own_block.wait()
+    for copy in own_blocks():
+        copy.wait()
     for shift in range(1, n):
-        block_copy(shift, source(shift)).wait_recv()
-
-    rows = jnp.zeros((8, total_rp), jnp.float32)
-    for slot in range(n):
-        placed = blocks[slot, q_local:, :]
-        rows = rows + (pltpu.roll(placed, slot * local_rp, 1) if slot else placed)
+        for copy in block_copies(shift, source(shift)):
+            copy.wait_recv()
+
     width = parts * total_rp
     repeat = lax.broadcasted_iota(jnp.int32, (total_rp, width), 1) // parts
     repeat = repeat == lax.broadcasted_iota(jnp.int32, (total_rp, width), 0)
-    rows = jnp.dot(rows, repeat.astype(jnp.float32), preferred_element_type=jnp.float32)
-    grid = rows.astype(jnp.int32)
-    turns = jnp.zeros((q_count, width), jnp.int32)
-    for axis in range(3):
-        turns = turns + ((points[:, axis : axis + 1] * grid[axis : axis + 1, :]) & (QGRID - 1))
-    turns = turns & (QGRID - 1)
-    weights = 1.0 / rows[3:4, :]
+    repeat = repeat.astype(jnp.bfloat16)
+
+    def twice(full):
+        row = jnp.concatenate([full[slot] for slot in range(n)], axis=1)
+        row = row.astype(jnp.float32).astype(jnp.bfloat16)
+        return jnp.dot(row, repeat, preferred_element_type=jnp.float32)
+
+    turns = lax.dot_general(
+        points[...].astype(jnp.float32).astype(jnp.bfloat16),
+        twice(all_coords).astype(jnp.bfloat16),
+        (((0,), (0,)), ((), ())),
+        preferred_element_type=jnp.float32,
+    )
+    turns = turns.astype(jnp.int32) & (QGRID - 1)
+    weights = 1.0 / twice(all_degeneracy)
     cos = pick(turns, column_of(0.0)) * weights
     sin = pick(turns, column_of(QGRID / 4)) * weights
     real_part = lax.rem(lax.broadcasted_iota(jnp.int32, (q_count, width), 1), parts) == 0
@@ -258,18 +280,13 @@
         [jnp.where(real_part, cos, -sin), jnp.where(real_part, sin, cos)], axis=0
     ).astype(jnp.bfloat16)
 
-    entries = parts * modes * modes
-
-    def spread(slot, carry):
-        held = blocks[slot, :q_local, :]
-        rows_at = pl.ds(pl.multiple_of(slot * q_local, q_local), q_local)
-        for entry in range(entries):
-            vectors[entry, rows_at, :] = jnp.broadcast_to(
-                held[:, entry : entry + 1], (q_local, lanes)
+    for part in range(parts):
+        placed = jnp.concatenate([all_eigvec[slot, :, part, :] for slot in range(n)], axis=1)
+        placed = jnp.transpose(placed)
+        for entry in range(modes * modes):
+            vectors[part * modes * modes + entry] = jnp.broadcast_to(
+                placed[:, entry : entry + 1], (q_count, lanes)
             )
-        return carry
-
-    lax.fori_loop(0, n, spread, 0)
 
     for turn, offset in enumerate(offsets):
         for mode in range(modes):
@@ -314,7 +331,8 @@
             send_first(offsets[turn + 2])
 
     for shift in range(1, n):
-        block_copy(shift, me).wait_send()
+        for copy in block_copies(shift, me):
+            copy.wait_send()
     for offset in offsets:
         for shift in range(n):
             if shift:
@@ -336,18 +354,12 @@
     total_rp = local_rp * n
     q_count = q_local * n
     entries = parts * modes * modes
-    stacked = jnp.concatenate([rp_coords, degeneracy[None, :]], axis=0).astype(jnp.float32)
-    block = jnp.concatenate(
-        [
-            jnp.pad(eigvec.reshape(q_local, entries), ((0, 0), (0, total_rp - entries))),
-            jnp.pad(stacked, ((0, 8 - stacked.shape[0]), (0, total_rp - local_rp))),
-        ],
-        axis=0,
-    )
     gathered = pl.pallas_call(
         functools.partial(exchange_kernel, n, planes),
         out_shape=jax.ShapeDtypeStruct((q_local, planes, modes, parts, n * lanes), jnp.bfloat16),
         in_specs=[
+            pl.BlockSpec(memory_space=pl.ANY),
+            pl.BlockSpec(memory_space=pl.ANY),
             pl.BlockSpec(memory_space=pl.ANY),
             pl.BlockSpec(memory_space=pl.ANY),
             pl.BlockSpec(memory_space=pltpu.VMEM),
@@ -355,21 +367,29 @@
         out_specs=pl.BlockSpec(memory_space=pl.ANY),
         scratch_shapes=[
             pltpu.VMEM((planes, modes, total_rp, parts, lanes), jnp.bfloat16),
-            pltpu.VMEM((n, q_local + 8, total_rp), jnp.float32),
+            pltpu.VMEM((n,) + rp_coords.shape, jnp.int32),
+            pltpu.VMEM((n, 1, local_rp), jnp.int32),
+            pltpu.VMEM((n, modes * modes, parts, q_local), jnp.float32),
             pltpu.VMEM((parts * q_count, modes * lanes), jnp.float32),
             pltpu.VMEM((entries, q_count, lanes), jnp.float32),
             pltpu.VMEM((q_count * modes * parts, lanes), jnp.float32),
             pltpu.VMEM((planes, q_count, modes, parts, lanes), jnp.bfloat16),
-            pltpu.SemaphoreType.DMA((planes * modes + 2,)),
-            pltpu.SemaphoreType.DMA((n,)),
-            pltpu.SemaphoreType.DMA((n,)),
+            pltpu.SemaphoreType.DMA((planes * modes + 4,)),
+            pltpu.SemaphoreType.DMA((n, 3)),
+            pltpu.SemaphoreType.DMA((n, 3)),
             pltpu.SemaphoreType.DMA((planes, n, modes)),
             pltpu.SemaphoreType.DMA((planes, n, modes)),
             pltpu.SemaphoreType.DMA((planes, n)),
             pltpu.SemaphoreType.DMA((planes, n)),
         ],
         compiler_params=pltpu.CompilerParams(collective_id=0, has_side_effects=True),
-    )(jnp.swapaxes(coupling[:, 0], 1, 2), block, qpoints.T)
+    )(
+        jnp.swapaxes(coupling[:, 0], 1, 2),
+        rp_coords,
+        degeneracy[None, :],
+        jnp.transpose(eigvec, (2, 3, 1, 0)).reshape(modes * modes, parts, q_local),
+        qpoints,
+    )
     return jnp.swapaxes(gathered, 2, 3).astype(jnp.float32)
 
 

time: 49.5 us -> 48.4 us (0.978)
  Pallas kernels: 42.3 us -> 45 us
  local copies, waits for them, and re-layouts: 2.38 us -> 0 us
  other arithmetic: 4.42 us -> 3.12 us
    pallas_call x1, Pallas kernels: 42.3 us -> 45 us  [exchanged(): pl.pallas_call(functools.partial(exchange_kernel, n, planes), out_shape=j...]
    unnamed x2 -> x0, local copies, waits for them, and re-layouts: 2.3 us -> none
    convert_element_type x1 -> x0, other arithmetic: 0.71 us -> none  [exchanged(): jnp.concatenate([rp_coords, degeneracy[None, :]], axis=0)]
    concatenate x1 -> x0, other arithmetic: 0.6 us -> none  [exchanged(): jnp.concatenate([jnp.pad(eigvec.reshape(q_local, entries), ((0, 0), (0, t...]
where the time goes in v3:
time: 48.4 us; the launch traced here: 48.1 us
  Pallas kernels  45 us (93%)
  other arithmetic  3.12 us (6%)
    pallas_call x1, Pallas kernels, exchanged(): pl.pallas_call(functools.partial(exchange_kernel, n, planes), out_shape=j...  45 us
    convert_element_type x1, other arithmetic, exchanged(): return jnp.swapaxes(gathered, 2, 3).astype(jnp.float32)  3.12 us

profile of v3, /device:TPU:0, one launch (start us, length us, event | category | flops | bytes accessed | tf_op | source)
XLA Modules:
  0.0 48.1 jit_solution(16613126338136107883)
XLA Ops:
  0.0 45.0 %shard_map.55 = bf16[8,4,6,2,1024]{4,3,2,1,0:T(2,128)(2,1)} custom-call(bf16[16,6,2,4096]{3,2,1,0:T(2,128)(2,1)} %bitcast.9, s32[3,16]{1,0:T(4,128)} %coords.1, s32[1,16]{1,0:T(1,128)} %bitcast.11, f32[36,2,8]{2,1,0:T(2,128)} %bitcast.10, s32[3,64]{1,0:T(4,128)} %points.1), custom_call_target="tpu_custom_call" | custom-call | tf_op jit(solution)/shard_map/pallas_call | solution.py:357
  45.0 3.1 %convert_bitcast_fusion = f32[8,4,2,6,1024]{4,2,3,1,0:T(2,128)} fusion(bf16[8,4,6,2,1024]{4,3,2,1,0:T(2,128)(2,1)} %shard_map.55), kind=kLoop, calls=%fused_computation | loop fusion | flops 393216 | bytes 2359296 | tf_op jit(solution)/shard_map/convert_element_type | solution.py:393

commit v4 on v3

--- a/solution.py
+++ b/solution.py
@@ -128,7 +128,7 @@
     local_rp, modes, parts, pairs = coupling.shape
     share = pairs // planes
     lanes = share // n
-    q_local = eigvec.shape[2]
+    q_local = eigvec.shape[0]
     q_count = n * q_local
     q_rows = q_local * modes * parts
     total_rp = n * local_rp
@@ -280,13 +280,9 @@
         [jnp.where(real_part, cos, -sin), jnp.where(real_part, sin, cos)], axis=0
     ).astype(jnp.bfloat16)
 
-    for part in range(parts):
-        placed = jnp.concatenate([all_eigvec[slot, :, part, :] for slot in range(n)], axis=1)
-        placed = jnp.transpose(placed)
-        for entry in range(modes * modes):
-            vectors[part * modes * modes + entry] = jnp.broadcast_to(
-                placed[:, entry : entry + 1], (q_count, lanes)
-            )
+    placed = all_eigvec[...].reshape(q_count, parts * modes * modes)
+    for entry in range(parts * modes * modes):
+        vectors[entry] = jnp.broadcast_to(placed[:, entry : entry + 1], (q_count, lanes))
 
     for turn, offset in enumerate(offsets):
         for mode in range(modes):
@@ -369,7 +365,7 @@
             pltpu.VMEM((planes, modes, total_rp, parts, lanes), jnp.bfloat16),
             pltpu.VMEM((n,) + rp_coords.shape, jnp.int32),
             pltpu.VMEM((n, 1, local_rp), jnp.int32),
-            pltpu.VMEM((n, modes * modes, parts, q_local), jnp.float32),
+            pltpu.VMEM((n, q_local, entries), jnp.float32),
             pltpu.VMEM((parts * q_count, modes * lanes), jnp.float32),
             pltpu.VMEM((entries, q_count, lanes), jnp.float32),
             pltpu.VMEM((q_count * modes * parts, lanes), jnp.float32),
@@ -387,7 +383,7 @@
         jnp.swapaxes(coupling[:, 0], 1, 2),
         rp_coords,
         degeneracy[None, :],
-        jnp.transpose(eigvec, (2, 3, 1, 0)).reshape(modes * modes, parts, q_local),
+        eigvec.reshape(q_local, entries),
         qpoints,
     )
     return jnp.swapaxes(gathered, 2, 3).astype(jnp.float32)

time: 48.4 us -> 47.3 us (0.977)
  Pallas kernels: 45 us -> 42.3 us
  local copies, waits for them, and re-layouts: 0 us -> 1.59 us
    pallas_call x1, Pallas kernels: 45 us -> 42.3 us  [exchanged(): pl.pallas_call(functools.partial(exchange_kernel, n, planes), out_shape=j...]
    unnamed x0 -> x1, local copies, waits for them, and re-layouts: none -> 0.91 us
    reshape x0 -> x1, local copies, waits for them, and re-layouts: none -> 0.68 us  [exchanged(): eigvec.reshape(q_local, entries)]
where the time goes in v4:
time: 47.3 us; the launch traced here: 47 us
  Pallas kernels  42.3 us (89%)
  other arithmetic  3.12 us (7%)
  local copies, waits for them, and re-layouts  1.59 us (3%)
    pallas_call x1, Pallas kernels, exchanged(): pl.pallas_call(functools.partial(exchange_kernel, n, planes), out_shape=j...  42.3 us
    convert_element_type x1, other arithmetic, exchanged(): return jnp.swapaxes(gathered, 2, 3).astype(jnp.float32)  3.12 us

profile of v4, /device:TPU:0, one launch (start us, length us, event | category | flops | bytes accessed | tf_op | source)
XLA Modules:
  0.0 47.0 jit_solution(129150240994441526)
XLA Ops:
  0.0 0.9 %copy.7 = f32[8,2,6,6]{3,2,1,0:T(8,128)S(1)} copy(f32[8,2,6,6]{0,1,3,2:T(2,128)} %param.9) | data formatting | bytes 4608 | tf_op args[4]
  0.9 0.7 %reshape.3.eigvec = f32[8,72]{1,0:T(8,128)} reshape(f32[8,2,6,6]{3,2,1,0:T(8,128)S(1)} %copy.7) | data formatting | bytes 4608 | tf_op jit(solution)/shard_map/reshape | solution.py:386
  1.6 42.3 %shard_map.55 = bf16[8,4,6,2,1024]{4,3,2,1,0:T(2,128)(2,1)} custom-call(bf16[16,6,2,4096]{3,2,1,0:T(2,128)(2,1)} %bitcast.6, s32[3,16]{1,0:T(4,128)} %coords.1, s32[1,16]{1,0:T(1,128)} %bitcast.7, f32[8,72]{1,0:T(8,128)} %reshape.3.eigvec, s32[3,64]{1,0:T(4,128)} %points.1), custom_call_target="tpu_custom_call" | custom-call | tf_op jit(solution)/shard_map/pallas_call | solution.py:353
  43.9 3.1 %convert_bitcast_fusion = f32[8,4,2,6,1024]{4,2,3,1,0:T(2,128)} fusion(bf16[8,4,6,2,1024]{4,3,2,1,0:T(2,128)(2,1)} %shard_map.55), kind=kLoop, calls=%fused_computation | loop fusion | flops 393216 | bytes 2359296 | tf_op jit(solution)/shard_map/convert_element_type | solution.py:389
